TPU v7x, 32 devices: a whole 2x2x4 slice. The times are simulated.
32 devices in a mesh: cp: 8 (over y, x, core), tp: 4 (over z).
Axes of the slice: x: 2, y: 2, z: 4, core: 2. Of those that a mesh axis runs over, the one named last changes fastest.
Arguments:
- queries: bfloat16 [6144, 5120], P('cp', 'tp'), may hold values from -36 to 36
- keys: bfloat16 [6144, 1024], P('cp', 'tp'), may hold values from -5 to 5
- values: bfloat16 [6144, 1024], P('cp', 'tp'), may hold values from -6 to 6
- doc_lengths: int32 [8], replicated, may hold values from 1 to 1536, 6144 in all
Outputs:
- attended: bfloat16 [6144, 5120], P(('cp', 'tp'))
Inputs may be any that keep to these rules, and one draw needn't show every extreme that they name: `doc_lengths`: they sum to 6144, and one of them is exactly 1536.
All inputs are finite; a program needn't handle non-finite values.
Results may differ from a plain program's by a relative error of at most 0.0038.
Values may be sent and summed in bfloat16 or wider, within the bound.
A program may use at most 256 MiB of HBM per device.

v0:
```python
import jax
import jax.numpy as jnp
from jax import lax
from jax.sharding import PartitionSpec as P

HEAD = 128
DOC_DEVS = 2


negative = -1e30


def doc_index(positions, doc_ends):
    return jnp.sum((positions[..., None] >= doc_ends).astype(jnp.int32), axis=-1)


def on_device(queries, keys, values, doc_lengths):
    tok_rows, q_cols = queries.shape
    kv_cols = keys.shape[1]
    kv_local = kv_cols // HEAD
    group_size = q_cols // kv_cols
    half_rows = tok_rows // 2
    cp_size = lax.axis_size("cp")
    my_index = lax.axis_index("cp")
    stretch_span = 2 * min(DOC_DEVS, cp_size // 2)
    doc_ends = jnp.cumsum(doc_lengths)
    paired = jnp.stack([keys, values])
    kv_bank = lax.all_gather(paired[None], "cp", axis=0, tiled=True)
    bank_slots = kv_bank.shape[0]
    kv_bank = kv_bank.reshape(bank_slots, 2, 2, half_rows, kv_local, HEAD)
    stretch_ids = jnp.stack([my_index, 2 * cp_size - 1 - my_index])
    offsets = jnp.arange(half_rows, dtype=jnp.int32)
    q_pos = stretch_ids[:, None] * half_rows + offsets[None, :]
    q_doc = doc_index(q_pos, doc_ends)
    q_blocks = queries.reshape(2, half_rows, kv_local, group_size, HEAD)
    scale = float(HEAD) ** (-0.5)

    def fetch_block(kv_slot, kv_part):
        kv_piece = lax.dynamic_index_in_dim(kv_bank, kv_slot, 0, keepdims=False)
        return lax.dynamic_index_in_dim(kv_piece, kv_part, 1, keepdims=False)

    def one_tile(tile_step, state_now):
        needed = stretch_ids - tile_step
        present = needed >= 0
        clamped = jnp.maximum(needed, 0)
        device_ids = jnp.where(clamped < cp_size, clamped, 2 * cp_size - 1 - clamped)
        kv_part = (clamped >= cp_size).astype(jnp.int32)
        kv_slot = jnp.clip(device_ids, 0, bank_slots - 1)
        k_pos = clamped[:, None] * half_rows + offsets[None, :]
        k_doc = doc_index(k_pos, doc_ends)
        allowed = (
            present[:, None, None]
            & (k_doc[:, None, :] == q_doc[:, :, None])
            & (k_pos[:, None, :] <= q_pos[:, :, None])
        )
        running_max, running_sum, running_out = state_now
        pieces = jnp.stack([fetch_block(kv_slot[which], kv_part[which]) for which in range(2)])
        scores = (
            jnp.einsum(
                "cqhjd,ckhd->cqhjk", q_blocks, pieces[:, 0], preferred_element_type=jnp.float32
            )
            * scale
        )
        allowed_wide = allowed[:, :, None, None, :]
        scores = jnp.where(allowed_wide, scores, negative)
        new_max = jnp.maximum(running_max, jnp.max(scores, axis=-1))
        weights = jnp.where(allowed_wide, jnp.exp(scores - new_max[..., None]), 0.0)
        rescale = jnp.exp(running_max - new_max)
        new_sum = rescale * running_sum + jnp.sum(weights, axis=-1)
        product = jnp.einsum(
            "cqhjk,ckhd->cqhjd",
            weights.astype(jnp.bfloat16),
            pieces[:, 1],
            preferred_element_type=jnp.float32,
        )
        new_out = rescale[..., None] * running_out + product
        return (new_max, new_sum, new_out)

    start_state = (
        jnp.full((2, half_rows, kv_local, group_size), negative, jnp.float32),
        jnp.zeros((2, half_rows, kv_local, group_size), jnp.float32),
        jnp.zeros((2, half_rows, kv_local, group_size, HEAD), jnp.float32),
    )
    final_max, final_sum, final_out = lax.fori_loop(0, stretch_span + 1, one_tile, start_state)
    attended = (final_out / final_sum[..., None]).reshape(tok_rows, q_cols).astype(jnp.bfloat16)
    return lax.all_to_all(attended, "tp", split_axis=0, concat_axis=1, tiled=True)


def solution(mesh):
    in_specs = (P("cp", "tp"), P("cp", "tp"), P("cp", "tp"), P())
    out_specs = P(("cp", "tp"), None)
    return jax.shard_map(
        on_device, mesh=mesh, in_specs=in_specs, out_specs=out_specs, check_vma=False
    )
```

profile of v0, /device:TPU:0, one launch (start us, length us, event | category | flops | bytes accessed | tf_op | source)
XLA Modules:
  0.0 252.6 jit_solution(6885560735671889990)
XLA Ops:
  6.5 2.1 pad_maximum_fusion.1
  9.5 5.7 %reshape.167 = bf16[2,384,2,5,128]{4,3,2,1,0:T(8,128)(2,1)} reshape(bf16[768,1280]{1,0:T(8,128)(2,1)} %param.6) | data formatting | bytes 3932160 | tf_op jit(solution)/shard_map/reshape | solution.py:35
  15.2 2.4 copy.32
  17.9 39.5 %all-gather.3.cloned.1.call-done = bf16[16,768,256]{2,1,0:T(8,128)(2,1)} async-done(((bf16[2,768,256]{2,1,0:T(8,128)(2,1)}), bf16[16,768,256]{2,1,0:T(8,128)(2,1)}) %all-gather.3.cloned.1.call-update) | async-done | bytes 6291472 | tf_op jit(solution)/shard_map/all_gather | solution.py:28
  57.4 9.8 %reshape.161 = bf16[8,2,2,384,2,128]{5,4,3,2,1,0:T(2,128)(2,1)} reshape(bf16[16,768,256]{2,1,0:T(8,128)(2,1)} %all-gather.3.cloned.1.call-done) | data formatting | bytes 12582912 | tf_op jit(solution)/shard_map/reshape | solution.py:30
  67.1 7.1 %copy.31 = bf16[8,2,2,384,2,128]{5,3,4,1,2,0:T(8,128)(2,1)} copy(bf16[8,2,2,384,2,128]{5,4,3,2,1,0:T(2,128)(2,1)} %reshape.161) | data formatting | bytes 12582912
  74.2 108.8 %while.21 = (s32[]{:T(128)}, f32[2,384,2,5]{1,3,2,0:T(8,128)S(1)}, f32[2,384,2,5]{1,3,2,0:T(8,128)S(1)}, f32[2,384,2,5,128]{1,4,3,2,0:T(8,128)}, s32[2]{0:T(128)...) while((s32[]{:T(128)}, f32[2,384,2,5]{1,3,2,0:T(8,128)S(1)}, ...), condition=%wide.region_6.7_spmd.clone, body=%wide.region_2.6_spmd.clone.sunk | while | flops 1554047232 | bytes 50061820 | solution.py:84
  84.5 2.0 fusion.42
  86.5 2.9 %fusion.43 = f32[2,384,2,5]{1,3,2,0:T(8,128)S(1)} fusion(f32[2,2,384,384,5]{3,2,4,1,0:T(8,128)S(1)} %get-tuple-element.508, f32[2,384,2,5]{1,3,2,0:T(8,128)S(1)} %select_maximum_fusion.2, pred[2,384,384]{1,2,0:T(8,128)(4,1)S(1)} %compare_and_fusion.2), kind=kLoop, calls=%fused_computation.6.clone.1 | loop fusion | flops 14737920 | bytes 12152832 | tf_op jit(solution)/shard_map/while/body/eval_jaxpr/reduce_sum | solution.py:69
  89.4 5.3 %bitcast_add_fusion.2 = f32[2,384,2,5,128]{1,4,3,2,0:T(8,128)} fusion(f32[2,384,2,5,128]{1,4,3,2,0:T(8,128)} %get-tuple-element.529, f32[2,2,384,384,5]{3,2,4,1,0:T(8,128)S(1)} %get-tuple-element.508, f32[2,384,2,5]{1,3,2,0:T(8,128)S(1)} %select_maximum_fusion.2, pred[2,384,384]{1,2,0:T(8,128)(4,1)S(1)} %compare_and_fusion.2, ...), kind=kOutput, calls=%fused_computation.9.clone.1 | convolution fusion | flops 773455872 | bytes 20803584 | tf_op jit(solution)/shard_map/while/body/eval_jaxpr/cqhjk,ckhd->cqhjd/dot_general | solution.py:70
  105.0 2.0 fusion.42
  107.1 2.9 %fusion.43 = f32[2,384,2,5]{1,3,2,0:T(8,128)S(1)} fusion(f32[2,2,384,384,5]{3,2,4,1,0:T(8,128)S(1)} %get-tuple-element.508, f32[2,384,2,5]{1,3,2,0:T(8,128)S(1)} %select_maximum_fusion.2, pred[2,384,384]{1,2,0:T(8,128)(4,1)S(1)} %compare_and_fusion.2), kind=kLoop, calls=%fused_computation.6.clone.1 | loop fusion | flops 14737920 | bytes 12152832 | tf_op jit(solution)/shard_map/while/body/eval_jaxpr/reduce_sum | solution.py:69
  110.0 6.8 %bitcast_add_fusion.2 = f32[2,384,2,5,128]{1,4,3,2,0:T(8,128)} fusion(f32[2,384,2,5,128]{1,4,3,2,0:T(8,128)} %get-tuple-element.529, f32[2,2,384,384,5]{3,2,4,1,0:T(8,128)S(1)} %get-tuple-element.508, f32[2,384,2,5]{1,3,2,0:T(8,128)S(1)} %select_maximum_fusion.2, pred[2,384,384]{1,2,0:T(8,128)(4,1)S(1)} %compare_and_fusion.2, ...), kind=kOutput, calls=%fused_computation.9.clone.1 | convolution fusion | flops 773455872 | bytes 20803584 | tf_op jit(solution)/shard_map/while/body/eval_jaxpr/cqhjk,ckhd->cqhjd/dot_general | solution.py:70
  127.1 2.0 fusion.42
  129.1 2.9 %fusion.43 = f32[2,384,2,5]{1,3,2,0:T(8,128)S(1)} fusion(f32[2,2,384,384,5]{3,2,4,1,0:T(8,128)S(1)} %get-tuple-element.508, f32[2,384,2,5]{1,3,2,0:T(8,128)S(1)} %select_maximum_fusion.2, pred[2,384,384]{1,2,0:T(8,128)(4,1)S(1)} %compare_and_fusion.2), kind=kLoop, calls=%fused_computation.6.clone.1 | loop fusion | flops 14737920 | bytes 12152832 | tf_op jit(solution)/shard_map/while/body/eval_jaxpr/reduce_sum | solution.py:69
  132.1 6.8 %bitcast_add_fusion.2 = f32[2,384,2,5,128]{1,4,3,2,0:T(8,128)} fusion(f32[2,384,2,5,128]{1,4,3,2,0:T(8,128)} %get-tuple-element.529, f32[2,2,384,384,5]{3,2,4,1,0:T(8,128)S(1)} %get-tuple-element.508, f32[2,384,2,5]{1,3,2,0:T(8,128)S(1)} %select_maximum_fusion.2, pred[2,384,384]{1,2,0:T(8,128)(4,1)S(1)} %compare_and_fusion.2, ...), kind=kOutput, calls=%fused_computation.9.clone.1 | convolution fusion | flops 773455872 | bytes 20803584 | tf_op jit(solution)/shard_map/while/body/eval_jaxpr/cqhjk,ckhd->cqhjd/dot_general | solution.py:70
  151.2 2.9 %fusion.43 = f32[2,384,2,5]{1,3,2,0:T(8,128)S(1)} fusion(f32[2,2,384,384,5]{3,2,4,1,0:T(8,128)S(1)} %get-tuple-element.508, f32[2,384,2,5]{1,3,2,0:T(8,128)S(1)} %select_maximum_fusion.2, pred[2,384,384]{1,2,0:T(8,128)(4,1)S(1)} %compare_and_fusion.2), kind=kLoop, calls=%fused_computation.6.clone.1 | loop fusion | flops 14737920 | bytes 12152832 | tf_op jit(solution)/shard_map/while/body/eval_jaxpr/reduce_sum | solution.py:69
  154.1 6.8 %bitcast_add_fusion.2 = f32[2,384,2,5,128]{1,4,3,2,0:T(8,128)} fusion(f32[2,384,2,5,128]{1,4,3,2,0:T(8,128)} %get-tuple-element.529, f32[2,2,384,384,5]{3,2,4,1,0:T(8,128)S(1)} %get-tuple-element.508, f32[2,384,2,5]{1,3,2,0:T(8,128)S(1)} %select_maximum_fusion.2, pred[2,384,384]{1,2,0:T(8,128)(4,1)S(1)} %compare_and_fusion.2, ...), kind=kOutput, calls=%fused_computation.9.clone.1 | convolution fusion | flops 773455872 | bytes 20803584 | tf_op jit(solution)/shard_map/while/body/eval_jaxpr/cqhjk,ckhd->cqhjd/dot_general | solution.py:70
  173.3 2.9 %fusion.43 = f32[2,384,2,5]{1,3,2,0:T(8,128)S(1)} fusion(f32[2,2,384,384,5]{3,2,4,1,0:T(8,128)S(1)} %get-tuple-element.508, f32[2,384,2,5]{1,3,2,0:T(8,128)S(1)} %select_maximum_fusion.2, pred[2,384,384]{1,2,0:T(8,128)(4,1)S(1)} %compare_and_fusion.2), kind=kLoop, calls=%fused_computation.6.clone.1 | loop fusion | flops 14737920 | bytes 12152832 | tf_op jit(solution)/shard_map/while/body/eval_jaxpr/reduce_sum | solution.py:69
  176.2 6.8 %bitcast_add_fusion.2 = f32[2,384,2,5,128]{1,4,3,2,0:T(8,128)} fusion(f32[2,384,2,5,128]{1,4,3,2,0:T(8,128)} %get-tuple-element.529, f32[2,2,384,384,5]{3,2,4,1,0:T(8,128)S(1)} %get-tuple-element.508, f32[2,384,2,5]{1,3,2,0:T(8,128)S(1)} %select_maximum_fusion.2, pred[2,384,384]{1,2,0:T(8,128)(4,1)S(1)} %compare_and_fusion.2, ...), kind=kOutput, calls=%fused_computation.9.clone.1 | convolution fusion | flops 773455872 | bytes 20803584 | tf_op jit(solution)/shard_map/while/body/eval_jaxpr/cqhjk,ckhd->cqhjd/dot_general | solution.py:70
  183.0 3.8 %divide_convert_fusion = bf16[2,384,2,5,128]{1,4,3,2,0:T(8,128)(2,1)} fusion(f32[2,384,2,5,128]{1,4,3,2,0:T(8,128)} %get-tuple-element.300, f32[2,384,2,5]{1,3,2,0:T(8,128)S(1)} %get-tuple-element.301), kind=kLoop, calls=%fused_computation.40 | loop fusion | flops 1966080 | bytes 5928960 | tf_op jit(solution)/shard_map/convert_element_type | solution.py:85
  186.8 3.8 %copy.41 = bf16[2,384,2,5,128]{4,3,2,1,0:T(8,128)(2,1)S(1)} copy(bf16[2,384,2,5,128]{1,4,3,2,0:T(8,128)(2,1)} %divide_convert_fusion) | data formatting | bytes 3932160 | tf_op jit(solution)/shard_map/convert_element_type | solution.py:85
  190.7 3.2 %reshape.168 = bf16[4,192,1280]{2,1,0:T(8,128)(2,1)} reshape(bf16[2,384,2,5,128]{4,3,2,1,0:T(8,128)(2,1)S(1)} %copy.41) | data formatting | bytes 3932160 | tf_op jit(solution)/shard_map/convert_element_type | solution.py:85
  193.9 50.4 %all_to_all.16 = bf16[4,192,1280]{2,1,0:T(8,128)(2,1)S(1)} all-to-all(bf16[4,192,1280]{2,1,0:T(8,128)(2,1)} %reshape.168), channel_id=1, replica_groups=mesh['cp'=8,'tp'=4] {'tp'}, dimensions={0} | all-to-all | bytes 3932160 | tf_op jit(solution)/shard_map/all_to_all | solution.py:86
  (67 shorter events, 21.5 us)
Async XLA Ops:
  6.5 50.8 %all-gather.3.cloned.1.call-start = ((), (), s32[]{:S(2)}) async-start(), calls=%async_computation.1 | async-start | bytes 7077888 | tf_op jit(solution)/shard_map/all_gather | solution.py:28
Sparse Core Ops, SparseCore 0:
  9.2 48.1 all-gather.2
where the time goes:
time: 254 us; the launch traced here: 253 us
  blocking collectives  50.4 us (20%)
  local copies, waits for them, and re-layouts  45.3 us (18%)
  matrix products  42.8 us (17%)
  waiting for transfers between devices  39.5 us (16%)
  loops' own time  36.9 us (15%)
  other arithmetic  24.3 us (10%)
  between operations  13.4 us (5%)
    all_to_all x1, blocking collectives, on_device(): lax.all_to_all(attended, 'tp', split_axis=0, concat_axis=1, tiled=True)  50.4 us
    all_gather x1, waiting for transfers between devices, on_device(): kv_bank = lax.all_gather(paired[None], 'cp', axis=0, tiled=True)  39.5 us
    another operation x1, loops' own time, on_device(): lax.fori_loop(0, stretch_span + 1, one_tile, start_state)  36.9 us
    dot_general x5, matrix products, one_tile(): jnp.einsum('cqhjk,ckhd->cqhjd', weights.astype(jnp.bfloat16), pieces[:, 1...  32.5 us
    reduce_sum x5, other arithmetic, one_tile(): new_sum = rescale * running_sum + jnp.sum(weights, axis=-1)  14.3 us
    dot_general x5, matrix products, one_tile(): jnp.einsum('cqhjd,ckhd->cqhjk', q_blocks, pieces[:, 0], preferred_element...  10.2 us
    reshape x1, local copies, waits for them, and re-layouts, on_device(): kv_bank = kv_bank.reshape(bank_slots, 2, 2, half_rows, kv_local, HEAD)  9.75 us
    unnamed x2, local copies, waits for them, and re-layouts  9.53 us
  transfers between devices with their start and end apart: 1, of which 1 were waited for; matrix products, arithmetic and copies ran while one was open for 4% of the time, Pallas kernels for 0%

commit v1 on v0

v1 whole, which is shorter than its diff:
```python
import functools
import math

import jax
import jax.numpy as jnp
from jax import lax
from jax.experimental import pallas as pl
from jax.experimental.pallas import tpu as pltpu
from jax.sharding import PartitionSpec as P

HEAD = 128
BACK = 4
LANES = 128
negative = -1e30
MESH = pl.DeviceIdType.MESH


def kernel(
    n_cp, n_tp, group, kv_local,
    doc_ref, q_ref, k_ref, v_ref, out_ref,
    kbuf, vbuf, bias_ref, s_ref, mx_ref, p_ref, obuf,
    own_send, relay_send, kv_recv, o_send, o_recv,
):
    tok = q_ref.shape[0]
    half = tok // 2
    rows = tok // n_tp
    parts = half // rows
    window = bias_ref.shape[2]
    step = half * (BACK + 1) - window
    step = step // max(parts - 1, 1)
    cols = group * HEAD
    me = lax.axis_index("cp")
    tp = lax.axis_index("tp")
    core = me % 2
    chip = me // 2
    chips = n_cp // 2
    partner = me + 1 - 2 * core
    bufs = (kbuf, vbuf)
    srcs = (k_ref, v_ref)
    idx = (core, 1 - core)

    def part(kv, h, g, slot):
        return bufs[kv][g].at[h, pl.ds(pl.multiple_of(slot * half, half), half)]

    def src(kv, h, g):
        return srcs[kv].at[pl.ds(h * half, half), pl.ds(g * HEAD, HEAD)]

    def send(source, kv, h, g, slot, ssem, dev):
        return pltpu.make_async_remote_copy(
            src_ref=source,
            dst_ref=part(kv, h, g, slot),
            send_sem=ssem,
            recv_sem=kv_recv.at[kv, h, g, slot],
            device_id={"cp": dev},
            device_id_type=MESH,
        )

    routes = []
    for o in (2, 1):
        base = (2 - o) * 2
        routes.append((0, o, chip + o <= chips - 1, chip + o, 0, base + idx[0]))
        if o == 2:
            routes.append((0, o, chip == chips - 1, chips - 2, 1, base + idx[0]))
        routes.append((1, o, chip >= o, chip - o, 1, base + idx[1]))

    def own_copies(g, fn):
        for kv in range(2):
            for h, o, when, tchip, thalf, slot in routes:
                @pl.when(when)
                def _(kv=kv, h=h, o=o, tchip=tchip, thalf=thalf, slot=slot):
                    fn(send(src(kv, h, g), kv, thalf, g, slot, own_send.at[kv, h, g, o], 2 * tchip + core))
            for h in range(2):
                fn(send(src(kv, h, g), kv, h, g, 4 + idx[h], own_send.at[kv, h, g, 0], partner))

    arrivals = []
    for o in (2, 1):
        arrivals.append((0, o, chip >= o, core))
        arrivals.append((1, o, chip < chips - o, 1 - core))
        if o == 2:
            arrivals.append((1, o, chip == chips - 2, core))

    def relays(g, fn):
        for h, o, when, r in arrivals:
            @pl.when(when)
            def _(h=h, o=o, r=r):
                for kv in range(2):
                    slot = (2 - o) * 2 + r
                    fn(send(part(kv, h, g, slot), kv, h, g, slot, relay_send.at[kv, h, g, o], partner))

    def take(copy):
        copy.wait_recv()
        copy.start()

    def relay_arrivals(g):
        for h, o, when, r in arrivals:
            @pl.when(when)
            def _(h=h, o=o, r=r):
                for kv in range(2):
                    slot = (2 - o) * 2 + 1 - r
                    send(part(kv, h, g, slot), kv, h, g, slot, relay_send.at[kv, h, g, o], partner).wait_recv()
        for h in range(2):
            for kv in range(2):
                slot = 4 + 1 - idx[h]
                send(part(kv, h, g, slot), kv, h, g, slot, own_send.at[kv, h, g, 0], partner).wait_recv()

        @pl.when(chip == chips - 1)
        def _():
            for buf in bufs:
                buf[g][1, 0:4 * half] = buf[g][0, 2 * half:6 * half]

    for g in range(kv_local):
        own_copies(g, lambda copy: copy.start())

    for g in range(kv_local):
        for h in range(2):
            for kv in range(2):
                part(kv, h, g, 4 + idx[h])[...] = srcs[kv][h * half:(h + 1) * half, g * HEAD:(g + 1) * HEAD]
        for lowest in range(2):
            @pl.when(chip <= lowest)
            def _(g=g, lowest=lowest):
                first = 2 if lowest == 0 else 0
                for buf in bufs:
                    buf[g][0, first * half:(first + 2) * half] = jnp.zeros((2 * half, HEAD), jnp.bfloat16)

    def place(u):
        h = u // parts
        i = u % parts
        pair = chip + h * (2 * chips - 1 - 2 * chip)
        index = core + h * (1 - 2 * core)
        return h, i, pair, index

    def make_bias(u, _):
        h, i, pair, index = place(u)
        block = 2 * pair + index
        q_pos = block * half + i * rows + lax.broadcasted_iota(jnp.int32, (rows, LANES), 0)

        def doc_step(j, carry):
            end, low = carry
            end = end + doc_ref[j]
            return end, jnp.where(end <= q_pos, end, low)

        _, low = lax.fori_loop(0, doc_ref.shape[0], doc_step, (jnp.int32(0), jnp.zeros((rows, LANES), jnp.int32)))
        first = (block - BACK) * half + i * step
        for tile in range(window // LANES):
            k_pos = first + tile * LANES + lax.broadcasted_iota(jnp.int32, (rows, LANES), 1)
            ok = (k_pos >= low) & (k_pos <= q_pos)
            bias_ref[u, :, tile * LANES:(tile + 1) * LANES] = jnp.where(ok, 0.0, negative)
        return 0

    lax.fori_loop(0, n_tp, make_bias, 0)

    chunk = 2 * LANES
    factor = float(HEAD) ** -0.5 * math.log2(math.e)

    def out_copy(g, u):
        return pltpu.make_async_remote_copy(
            src_ref=obuf.at[g, u],
            dst_ref=out_ref.at[:, pl.ds(pl.multiple_of(tp * (kv_local * cols) + g * cols, LANES), cols)],
            send_sem=o_send.at[g, u],
            recv_sem=o_recv.at[g, tp],
            device_id={"tp": u},
            device_id_type=MESH,
        )

    def out_arrival(g, source):
        return pltpu.make_async_remote_copy(
            src_ref=obuf.at[g, source],
            dst_ref=out_ref.at[:, pl.ds(pl.multiple_of(source * (kv_local * cols) + g * cols, LANES), cols)],
            send_sem=o_send.at[g, source],
            recv_sem=o_recv.at[g, source],
            device_id={"tp": source},
            device_id_type=MESH,
        )

    def attend(g, u):
        h, i, pair, index = place(u)
        row0 = pl.multiple_of(u * rows, 16)
        q = jnp.concatenate(
            [q_ref[pl.ds(row0, rows), (g * group + j) * HEAD:(g * group + j + 1) * HEAD] for j in range(group)], axis=0
        )
        start = index * half + i * step
        mx_ref[...] = jnp.full(mx_ref.shape, negative, jnp.float32)

        def score_chunk(kc, _):
            k = kbuf[g][h, pl.ds(pl.multiple_of(start + kc * chunk, LANES), chunk), :]
            s = lax.dot_general(q, k, (((1,), (1,)), ((), ())), preferred_element_type=jnp.float32)
            at = pl.ds(pl.multiple_of(kc * chunk, chunk), chunk)
            bias = bias_ref[u, :, at]
            for j in range(group):
                here = slice(j * rows, (j + 1) * rows)
                sj = s[here] + bias
                s_ref[here, at] = sj
                mx_ref[here] = jnp.maximum(mx_ref[here], jnp.maximum(sj[:, :LANES], sj[:, LANES:]))
            return 0

        lax.fori_loop(0, window // chunk, score_chunk, 0)
        tall = 64

        def weigh(rc, _):
            at = pl.ds(pl.multiple_of(rc * tall, tall), tall)
            top = jnp.max(mx_ref[at, :], axis=1, keepdims=True)
            p_ref[at, :] = jnp.exp2((s_ref[at, :] - top) * factor).astype(jnp.bfloat16)
            return 0

        lax.fori_loop(0, group * rows // tall, weigh, 0)
        v = vbuf[g][h, pl.ds(pl.multiple_of(start, LANES), window), :]
        wide = jnp.concatenate([v, jnp.ones_like(v)], axis=1)
        acc = jnp.dot(p_ref[...], wide, preferred_element_type=jnp.float32)
        done = (acc[:, :HEAD] / acc[:, HEAD:]).astype(jnp.bfloat16)
        for j in range(group):
            obuf[g, u, :, j * HEAD:(j + 1) * HEAD] = done[j * rows:(j + 1) * rows]

    relays(0, take)
    relay_arrivals(0)
    for g in range(kv_local):
        def one(k, _, g=g):
            u = (tp + 1 + k) % n_tp
            if g + 1 < kv_local:
                @pl.when(k == n_tp - 1)
                def _():
                    relays(g + 1, take)
            attend(g, u)

            @pl.when(k < n_tp - 1)
            def _():
                out_copy(g, u).start()
            return 0

        lax.fori_loop(0, n_tp, one, 0)
        out_ref[:, pl.ds(pl.multiple_of(tp * (kv_local * cols) + g * cols, LANES), cols)] = obuf[g, tp]
        if g + 1 < kv_local:
            relay_arrivals(g + 1)

    for g in range(kv_local):
        own_copies(g, lambda copy: copy.wait_send())
        relays(g, lambda copy: copy.wait_send())

        def finish(k, _, g=g):
            u = (tp + 1 + k) % n_tp
            out_copy(g, u).wait_send()
            out_arrival(g, u).wait_recv()
            return 0

        lax.fori_loop(0, n_tp - 1, finish, 0)


def on_device(queries, keys, values, doc_lengths):
    tok, q_cols = queries.shape
    kv_local = keys.shape[1] // HEAD
    group = q_cols // keys.shape[1]
    n_cp = lax.axis_size("cp")
    n_tp = lax.axis_size("tp")
    half = tok // 2
    rows = tok // n_tp
    window = -(-(BACK * half + rows) // (2 * LANES)) * 2 * LANES
    vmem = pl.BlockSpec(memory_space=pltpu.VMEM)
    dma = pltpu.SemaphoreType.DMA
    halo = (pltpu.VMEM((2, 6 * half, HEAD), jnp.bfloat16),) * kv_local
    return pl.pallas_call(
        functools.partial(kernel, n_cp, n_tp, group, kv_local),
        out_shape=jax.ShapeDtypeStruct((rows, q_cols * n_tp), jnp.bfloat16),
        in_specs=[pl.BlockSpec(memory_space=pltpu.SMEM), vmem, vmem, vmem],
        out_specs=vmem,
        scratch_shapes=[
            halo,
            halo,
            pltpu.VMEM((n_tp, rows, window), jnp.float32),
            pltpu.VMEM((group * rows, window), jnp.float32),
            pltpu.VMEM((group * rows, LANES), jnp.float32),
            pltpu.VMEM((group * rows, window), jnp.bfloat16),
            pltpu.VMEM((kv_local, n_tp, rows, group * HEAD), jnp.bfloat16),
            dma((2, 2, kv_local, 3)),
            dma((2, 2, kv_local, 3)),
            dma((2, 2, kv_local, 6)),
            dma((kv_local, n_tp)),
            dma((kv_local, n_tp)),
        ],
        compiler_params=pltpu.CompilerParams(has_side_effects=True, vmem_limit_bytes=60 * 1024 * 1024),
    )(doc_lengths, queries, keys, values)


def solution(mesh):
    in_specs = (P("cp", "tp"), P("cp", "tp"), P("cp", "tp"), P())
    return jax.shard_map(
        on_device, mesh=mesh, in_specs=in_specs, out_specs=P(("cp", "tp"), None), check_vma=False
    )
```

time: 254 us -> 76.9 us (0.30)
  Pallas kernels: 0 us -> 73.7 us
  blocking collectives: 50.4 us -> 0 us
  matrix products: 42.8 us -> 0 us
  local copies, waits for them, and re-layouts: 45.3 us -> 2.94 us
  waiting for transfers between devices: 39.5 us -> 0 us
  loops' own time: 36.9 us -> 0 us
  other arithmetic: 24.3 us -> 0 us
  between operations: 13.4 us -> 0.01 us
    pallas_call x0 -> x1, Pallas kernels: none -> 73.7 us  [on_device(): pl.pallas_call(functools.partial(kernel, n_cp, n_tp, group, kv_local), ou...]
    all_to_all x1 -> x0, blocking collectives: 50.4 us -> none  [on_device(): lax.all_to_all(attended, 'tp', split_axis=0, concat_axis=1, tiled=True)]
    dot_general x10 -> x0, matrix products: 42.8 us -> none  [the longest x5 32.5 us: one_tile(): jnp.einsum('cqhjk,ckhd->cqhjd', weights.astype(jnp.bfloat16), pieces[:, 1...]
    all_gather x1 -> x0, waiting for transfers between devices: 39.5 us -> none  [on_device(): kv_bank = lax.all_gather(paired[None], 'cp', axis=0, tiled=True)]
    another operation x1 -> x0, loops' own time: 36.9 us -> none  [on_device(): lax.fori_loop(0, stretch_span + 1, one_tile, start_state)]
    reshape x2 -> x0, local copies, waits for them, and re-layouts: 15.4 us -> none  [the longest x1 9.75 us: on_device(): kv_bank = kv_bank.reshape(bank_slots, 2, 2, half_rows, kv_local, HEAD)]
    reduce_sum x11 -> x0, other arithmetic: 14.8 us -> none  [the longest x5 14.3 us: one_tile(): new_sum = rescale * running_sum + jnp.sum(weights, axis=-1)]
    convert_element_type x2 -> x0, local copies, waits for them, and re-layouts: 7.04 us -> none  [on_device(): (final_out / final_sum[..., None]).reshape(tok_rows, q_cols)]
  transfers between devices with their start and end apart: 1 -> 0, of which waited for: 1 -> 0; matrix products, arithmetic and copies ran while one was open for 4% -> 0% of each run, Pallas kernels for 0% -> 0%
where the time goes in v1:
time: 76.9 us; the launch traced here: 76.6 us
  Pallas kernels  73.7 us (96%)
  local copies, waits for them, and re-layouts  2.94 us (4%)
    pallas_call x1, Pallas kernels, on_device(): pl.pallas_call(functools.partial(kernel, n_cp, n_tp, group, kv_local), ou...  73.7 us
    unnamed x1, local copies, waits for them, and re-layouts  2.94 us

profile of v1, /device:TPU:0, one launch (start us, length us, event | category | flops | bytes accessed | tf_op | source)
XLA Modules:
  0.0 76.6 jit_solution(18146659145091678826)
XLA Ops:
  0.0 73.7 %shard_map.46 = bf16[192,5120]{1,0:T(8,128)(2,1)} custom-call(s32[8]{0:T(128)} %doc_ref.1, bf16[768,1280]{1,0:T(8,128)(2,1)} %q_ref.1, bf16[768,256]{1,0:T(8,128)(2,1)} %k_ref.1, bf16[768,256]{1,0:T(8,128)(2,1)} %v_ref.1), custom_call_target="tpu_custom_call" | custom-call | tf_op jit(solution)/shard_map/pallas_call | solution.py:259
  73.7 2.9 %copy.6 = bf16[192,5120]{1,0:T(8,128)(2,1)} copy(bf16[192,5120]{1,0:T(8,128)(2,1)} %shard_map.46) | data formatting | bytes 3932160

commit v2 on v1

--- a/solution.py
+++ b/solution.py
@@ -108,8 +108,22 @@
             for buf in bufs:
                 buf[g][1, 0:4 * half] = buf[g][0, 2 * half:6 * half]
 
-    for g in range(kv_local):
-        own_copies(g, lambda copy: copy.start())
+    barrier = pltpu.get_barrier_semaphore()
+    greeted = n_tp
+    pl.semaphore_signal(barrier, inc=1, device_id={"cp": partner}, device_id_type=MESH)
+    for other in range(1, n_tp):
+        pl.semaphore_signal(barrier, inc=1, device_id={"tp": (tp + other) % n_tp}, device_id_type=MESH)
+    for away in (-2, -1, 1, 2):
+        there = chip + away
+        inside = (there >= 0) & (there < chips)
+        greeted = greeted + inside.astype(jnp.int32)
+
+        @pl.when(inside)
+        def _(there=there):
+            pl.semaphore_signal(barrier, inc=1, device_id={"cp": 2 * there + core}, device_id_type=MESH)
+    pl.semaphore_wait(barrier, greeted)
+
+    own_copies(0, lambda copy: copy.start())
 
     for g in range(kv_local):
         for h in range(2):
@@ -210,11 +224,19 @@
         for j in range(group):
             obuf[g, u, :, j * HEAD:(j + 1) * HEAD] = done[j * rows:(j + 1) * rows]
 
+    def order(k):
+        if n_tp != 4:
+            return (tp + 1 + k) % n_tp
+        far = (tp // 2 + 1 - k // 2) % 2
+        return 2 * far + (tp % 2 + k + k // 2) % 2
+
     relays(0, take)
+    for g in range(1, kv_local):
+        own_copies(g, lambda copy: copy.start())
     relay_arrivals(0)
     for g in range(kv_local):
         def one(k, _, g=g):
-            u = (tp + 1 + k) % n_tp
+            u = order(k)
             if g + 1 < kv_local:
                 @pl.when(k == n_tp - 1)
                 def _():
@@ -275,7 +297,7 @@
             dma((kv_local, n_tp)),
             dma((kv_local, n_tp)),
         ],
-        compiler_params=pltpu.CompilerParams(has_side_effects=True, vmem_limit_bytes=60 * 1024 * 1024),
+        compiler_params=pltpu.CompilerParams(has_side_effects=True, collective_id=0, vmem_limit_bytes=60 * 1024 * 1024),
     )(doc_lengths, queries, keys, values)
 
 

time: 76.9 us -> 72.8 us (0.947)
  Pallas kernels: 73.7 us -> 69.6 us
    pallas_call x1, Pallas kernels: 73.7 us -> 69.6 us  [on_device(): pl.pallas_call(functools.partial(kernel, n_cp, n_tp, group, kv_local), ou...]
where the time goes in v2:
time: 72.8 us; the launch traced here: 72.6 us
  Pallas kernels  69.6 us (96%)
  local copies, waits for them, and re-layouts  2.94 us (4%)
    pallas_call x1, Pallas kernels, on_device(): pl.pallas_call(functools.partial(kernel, n_cp, n_tp, group, kv_local), ou...  69.6 us
    unnamed x1, local copies, waits for them, and re-layouts  2.94 us

profile of v2, /device:TPU:0, one launch (start us, length us, event | category | flops | bytes accessed | tf_op | source)
XLA Modules:
  0.0 72.6 jit_solution(5954568007522005618)
XLA Ops:
  0.0 69.6 %shard_map.46 = bf16[192,5120]{1,0:T(8,128)(2,1)} custom-call(s32[8]{0:T(128)} %doc_ref.1, bf16[768,1280]{1,0:T(8,128)(2,1)} %q_ref.1, bf16[768,256]{1,0:T(8,128)(2,1)} %k_ref.1, bf16[768,256]{1,0:T(8,128)(2,1)} %v_ref.1), custom_call_target="tpu_custom_call" | custom-call | tf_op jit(solution)/shard_map/pallas_call | solution.py:281
  69.6 2.9 %copy.6 = bf16[192,5120]{1,0:T(8,128)(2,1)} copy(bf16[192,5120]{1,0:T(8,128)(2,1)} %shard_map.46) | data formatting | bytes 3932160

commit v3 on v2

--- a/solution.py
+++ b/solution.py
@@ -297,7 +297,7 @@
             dma((kv_local, n_tp)),
             dma((kv_local, n_tp)),
         ],
-        compiler_params=pltpu.CompilerParams(has_side_effects=True, collective_id=0, vmem_limit_bytes=60 * 1024 * 1024),
+        compiler_params=pltpu.CompilerParams(has_side_effects=True, collective_id=0, vmem_limit_bytes=44 * 1024 * 1024),
     )(doc_lengths, queries, keys, values)
 
 

time: 72.8 us -> 73 us (level)
  local copies, waits for them, and re-layouts: 2.94 us -> 5.46 us
  Pallas kernels: 69.6 us -> 67.2 us
    unnamed x1 -> x9, local copies, waits for them, and re-layouts: 2.94 us -> 5.46 us
    pallas_call x1, Pallas kernels: 69.6 us -> 67.2 us  [on_device(): pl.pallas_call(functools.partial(kernel, n_cp, n_tp, group, kv_local), ou...]
where the time goes in v3:
time: 73 us; the launch traced here: 72.7 us
  Pallas kernels  67.2 us (92%)
  local copies, waits for them, and re-layouts  5.46 us (7%)
    pallas_call x1, Pallas kernels, on_device(): pl.pallas_call(functools.partial(kernel, n_cp, n_tp, group, kv_local), ou...  67.2 us
    unnamed x9, local copies, waits for them, and re-layouts  5.46 us

profile of v3, /device:TPU:0, one launch (start us, length us, event | category | flops | bytes accessed | tf_op | source)
XLA Modules:
  0.0 72.7 jit_solution(11181659008068193366)
XLA Ops:
  0.0 0.0 copy-start
  0.0 1.5 %copy-done = bf16[768,1280]{1,0:T(8,128)(2,1)S(1)} copy-done((bf16[768,1280]{1,0:T(8,128)(2,1)S(1)}, bf16[768,1280]{1,0:T(8,128)(2,1)}, u32[]{:S(2)}) %copy-start) | copy-done | bytes 1966104
  1.5 0.0 copy-start.1
  1.5 1.0 %copy-done.1 = bf16[768,256]{1,0:T(8,128)(2,1)S(1)} copy-done((bf16[768,256]{1,0:T(8,128)(2,1)S(1)}, bf16[768,256]{1,0:T(8,128)(2,1)}, u32[]{:S(2)}) %copy-start.1) | copy-done | bytes 393240
  2.5 0.0 copy-start.2
  2.5 1.0 %copy-done.2 = bf16[768,256]{1,0:T(8,128)(2,1)S(1)} copy-done((bf16[768,256]{1,0:T(8,128)(2,1)S(1)}, bf16[768,256]{1,0:T(8,128)(2,1)}, u32[]{:S(2)}) %copy-start.2) | copy-done | bytes 393240
  3.5 0.0 copy-start.3
  3.5 0.7 copy-done.3
  4.2 67.2 %shard_map.46 = bf16[192,5120]{1,0:T(8,128)(2,1)S(1)} custom-call(s32[8]{0:T(128)S(1)} %copy-done.3, bf16[768,1280]{1,0:T(8,128)(2,1)S(1)} %copy-done, bf16[768,256]{1,0:T(8,128)(2,1)S(1)} %copy-done.1, bf16[768,256]{1,0:T(8,128)(2,1)S(1)} %copy-done.2), custom_call_target="tpu_custom_call" | custom-call | tf_op jit(solution)/shard_map/pallas_call | solution.py:281
  71.4 1.3 %copy.6 = bf16[192,5120]{1,0:T(8,128)(2,1)} copy(bf16[192,5120]{1,0:T(8,128)(2,1)S(1)} %shard_map.46) | data formatting | bytes 3932160
Async XLA Ops:
  0.0 1.5 %copy-start = (bf16[768,1280]{1,0:T(8,128)(2,1)S(1)}, bf16[768,1280]{1,0:T(8,128)(2,1)}, u32[]{:S(2)}) copy-start(bf16[768,1280]{1,0:T(8,128)(2,1)} %q_ref.1) | copy-start | bytes 5898244
  1.5 1.0 %copy-start.1 = (bf16[768,256]{1,0:T(8,128)(2,1)S(1)}, bf16[768,256]{1,0:T(8,128)(2,1)}, u32[]{:S(2)}) copy-start(bf16[768,256]{1,0:T(8,128)(2,1)} %k_ref.1) | copy-start | bytes 1179652
  2.5 1.0 %copy-start.2 = (bf16[768,256]{1,0:T(8,128)(2,1)S(1)}, bf16[768,256]{1,0:T(8,128)(2,1)}, u32[]{:S(2)}) copy-start(bf16[768,256]{1,0:T(8,128)(2,1)} %v_ref.1) | copy-start | bytes 1179652
  3.5 0.7 copy-start.3
